TPU v7x, 32 devices: a whole 2x2x4 slice. The times are simulated.
32 devices in a mesh: scene: 2 (over y), cam: 16 (over z, x, core).
Axes of the slice: x: 2, y: 2, z: 4, core: 2. Of those that a mesh axis runs over, the one named last changes fastest.
Arguments:
- queries: bfloat16 [32, 768, 1024], P(('scene', 'cam')), parts along dimension 0, may hold values from -32 to 32
- keys: bfloat16 [32, 768, 1024], P(('scene', 'cam')), parts along dimension 0, may hold values from -32 to 32
- values: bfloat16 [32, 768, 1024], P(('scene', 'cam')), parts along dimension 0, may hold values from -6 to 6
- residual: bfloat16 [32, 768, 1024], P(('scene', 'cam')), parts along dimension 0, may hold values from -1.5 to 1.5
- w_out: bfloat16 [1024, 1024], replicated, may hold values from -0.1875 to 0.1875
- neighbours: int32 [32, 4], P(('scene', 'cam')), parts along dimension 0, may hold values from 0 to 15, as said below
- band_start: int32 [32, 4], P(('scene', 'cam')), parts along dimension 0, may hold values from 0 to 3
- band_blocks: int32 [32, 4, 6, 2], P(('scene', 'cam')), parts along dimension 0, may hold values from 0 to 2, as said below
- band_count: int32 [32, 4, 6], P(('scene', 'cam')), parts along dimension 0, may hold values from 1 to 2, as said below
Outputs:
- output: bfloat16 [32, 768, 1024], P(('scene', 'cam')), parts along dimension 0
There are 2 independent parts, one for each index of `scene`. A program takes and returns all parts, laid end to end along the dimension named above; an argument that names none is the same for every part. Nothing has to cross between parts.
Inputs may be any that keep to these rules, and one draw needn't show every extreme that they name: `neighbours`: row v lists the views (v + k) mod 16 for k = 1, -1, 2, -2, each once, in an order drawn for each row. `band_blocks`: each list holds 2 different numbers; entries at positions band_count or later are not read. `band_count`: query block 0 of every slot has 2.
All inputs are finite; a program needn't handle non-finite values.
Results may differ from a plain program's by a relative error of at most 0.008.
Values may be sent and summed in bfloat16 or wider, within the bound.
A program may use at most 128 MiB of HBM per device.

v0:
```python
import functools
import math

import jax
import jax.numpy as jnp
from jax import lax
from jax.experimental import pallas as pl
from jax.experimental.pallas import tpu as pltpu
from jax.sharding import PartitionSpec as P

HEADS = 16
LANES = 128
ROLES = 4
HIDDEN = -1e30


def relays(cameras, rigs, qblocks):
    return rigs == 1 and cameras % 4 == 0 and qblocks % 2 == 0


def kernel(cfg, q_hbm, k_hbm, v_hbm, near_ref, start_ref, block_ref, count_ref, out_ref, *scratch):
    cameras, rigs, chunks, qblocks, most, head_dim = cfg
    relay = relays(cameras, rigs, qblocks)
    buffers = [scratch[r * chunks:(r + 1) * chunks] for r in range(ROLES)]
    q_ref, k_ref, v_ref, own_sem, first_send, first_recv, next_send, next_recv = scratch[ROLES * chunks:]
    part_a, part_b, part_x, part_z = range(ROLES)
    block_len = q_ref.shape[1]
    me = lax.axis_index("cam")

    def at(offset):
        return lax.rem(me + offset + 2 * cameras, cameras)

    if relay:
        column = lax.rem(me // 2, 2)
        core = lax.rem(me, 2)
        partner = me + 1 - 2 * core
        across = me + 2 - 4 * column
        z_to = at(4 - 8 * column)
        z_from = at(8 * column - 4)
        from_x = lax.rem(column + core, 2) == 0
        z_view = at(4 * column - 2)
        partner_x = partner + 2 - 4 * column
        partner_z = lax.rem(partner + 4 * column - 2 + cameras, cameras)
        b_view = jnp.where(from_x, partner_z, partner_x)
        views = (partner, b_view, across, z_view)
        peers = (partner, across, z_to, z_from)
        first = ((part_x, across), (part_a, partner))
    else:
        views = (at(rigs), at(-rigs), at(2 * rigs), at(-2 * rigs))
        peers = views
        first = (
            (part_a, views[1]), (part_b, views[0]), (part_x, views[3]), (part_z, views[2])
        )

    own_copies = [
        pltpu.make_async_copy(src, dst, own_sem.at[n])
        for n, (src, dst) in enumerate(((q_hbm, q_ref), (k_hbm, k_ref), (v_hbm, v_ref)))
    ]
    for copy in own_copies:
        copy.start()
    barrier = pltpu.get_barrier_semaphore()
    for peer in peers:
        pl.semaphore_signal(
            barrier, inc=1, device_id={"cam": peer}, device_id_type=pl.DeviceIdType.MESH
        )
    pl.semaphore_wait(barrier, len(peers))

    def first_copy(lane, g, kind, rows):
        role, target = first[lane]
        source = (v_hbm if isinstance(kind, int) and kind == 1 else k_hbm)
        part = kind * (qblocks // rows.size) + rows.start // rows.size
        return pltpu.make_async_remote_copy(
            src_ref=source.at[rows, :, pl.ds(g * LANES, LANES)],
            dst_ref=buffers[role][g].at[kind, rows],
            send_sem=first_send.at[lane, g, part],
            recv_sem=first_recv.at[lane, g, part],
            device_id={"cam": target},
            device_id_type=pl.DeviceIdType.MESH,
        )

    def next_copy(role, g, source_role, target, part):
        kind, rows = piece(part)
        return pltpu.make_async_remote_copy(
            src_ref=buffers[source_role][g].at[kind, rows],
            dst_ref=buffers[role][g].at[kind, rows],
            send_sem=next_send.at[role // 2, g, part],
            recv_sem=next_recv.at[role // 2, g, part],
            device_id={"cam": target},
            device_id_type=pl.DeviceIdType.MESH,
        )

    splits = qblocks // 2 if relay else 1

    def piece(part):
        return part // splits, pl.ds((part % splits) * (qblocks // splits), qblocks // splits)

    whole = pl.ds(0, qblocks)

    def first_parts(lane):
        if relay and lane == 0:
            return [piece(part) for part in range(2 * splits)]
        return [(kind, whole) for kind in range(2)]

    for lane in range(len(first)):
        for g in range(chunks):
            for kind, rows in first_parts(lane):
                first_copy(lane, g, kind, rows).start()

    def first_wait(lane, g):
        for kind, rows in first_parts(lane):
            first_copy(lane, g, kind, rows).wait_recv()

    slots = []
    for view in views:
        slot = jnp.int32(0)
        for s in range(1, ROLES):
            slot = jnp.where(near_ref[0, s] == view, s, slot)
        slots.append(slot)
    starts = [start_ref[0, slot] for slot in slots]

    def block_of(g):
        cols = slice(g * LANES, (g + 1) * LANES)

        def one_block(b, carry):
            heads = LANES // head_dim
            q = q_ref[b, :, cols] * jnp.asarray(1.0 / math.sqrt(head_dim), jnp.bfloat16)
            lane = lax.broadcasted_iota(jnp.int32, (block_len, LANES), 1) // head_dim
            q2 = jnp.concatenate(
                [jnp.where(lane == h, q, jnp.zeros_like(q)) for h in range(heads)], axis=0
            )
            dims = (((1,), (1,)), ((), ()))
            scores = [
                lax.dot_general(q2, k_ref[b, :, cols], dims, preferred_element_type=jnp.float32)
            ]
            vals = [v_ref[b, :, cols]]
            for r in range(ROLES):
                buffer = buffers[r][g]
                key_parts, val_parts, bias = [], [], []
                live = count_ref[0, slots[r], b]
                for m in range(most):
                    near = starts[r] + block_ref[0, slots[r], b, m]
                    if m > 0:
                        near = jnp.where(m < live, near, 0)
                        bias.append(jnp.where(m < live, 0.0, HIDDEN))
                    key_parts.append(buffer[0, near])
                    val_parts.append(buffer[1, near])
                got = lax.dot_general(
                    q2,
                    jnp.concatenate(key_parts, axis=0),
                    dims,
                    preferred_element_type=jnp.float32,
                )
                pieces = [got[:, :block_len]]
                for m in range(1, most):
                    pieces.append(got[:, m * block_len:(m + 1) * block_len] + bias[m - 1])
                scores.append(jnp.concatenate(pieces, axis=1))
                vals.append(jnp.concatenate(val_parts, axis=0))
            all_scores = jnp.concatenate(scores, axis=1)
            top = jnp.max(all_scores, axis=1, keepdims=True)
            expo = jnp.exp(all_scores - top)
            total = jnp.sum(expo, axis=1, keepdims=True)
            mixed = jnp.dot(
                expo.astype(jnp.bfloat16),
                jnp.concatenate(vals, axis=0),
                preferred_element_type=jnp.float32,
            )
            mixed = mixed / total
            result = mixed[:block_len]
            for h in range(1, heads):
                result = jnp.where(lane == h, mixed[h * block_len:(h + 1) * block_len], result)
            out_ref[b, :, cols] = result.astype(out_ref.dtype)
            return carry

        return one_block

    def compute(g, unroll):
        lax.fori_loop(0, qblocks, block_of(g), 0, unroll=unroll)

    if relay:

        def z_send(g, part):
            return next_copy(part_z, g, part_x, z_to, part)

        def b_send(g, source, part):
            return next_copy(part_b, g, source, partner, part)

        def after_x(g, part):
            first_copy(0, g, *piece(part)).wait_recv()
            z_send(g, part).start()

            @pl.when(from_x)
            def _():
                b_send(g, part_x, part).start()

        def after_z(g, part):
            z_send(g, part).wait_recv()

            @pl.when(jnp.logical_not(from_x))
            def _():
                b_send(g, part_z, part).start()

        def arrive(g):
            first_wait(1, g)

            def one_part(part, carry):
                b_send(g, part_x, part).wait_recv()
                return carry

            lax.fori_loop(0, qblocks, one_part, 0)

        for step in range(chunks + 1):
            if step == 2 or step == chunks < 2:
                for copy in own_copies:
                    copy.wait()
            done = step - 2 if step < chunks else chunks - 2
            if done >= 0:
                arrive(done)

            def one_part(part, carry):
                if step < chunks:
                    after_x(step, part)
                if step >= 1:
                    after_z(step - 1, part)
                if done >= 0:
                    block_of(done)(part, carry)
                return carry

            lax.fori_loop(0, qblocks, one_part, 0)
        arrive(chunks - 1)
        compute(chunks - 1, 3 if qblocks % 3 == 0 else 1)

        for g in range(chunks):

            def one_part(part, carry):
                z_send(g, part).wait_send()

                @pl.when(from_x)
                def _():
                    b_send(g, part_x, part).wait_send()

                @pl.when(jnp.logical_not(from_x))
                def _():
                    b_send(g, part_z, part).wait_send()

                return carry

            lax.fori_loop(0, qblocks, one_part, 0)
    else:
        for copy in own_copies:
            copy.wait()
        for g in range(chunks):
            for lane in range(len(first)):
                first_wait(lane, g)
            compute(g, 1)
    for lane in range(len(first)):
        for g in range(chunks):
            for kind, rows in first_parts(lane):
                first_copy(lane, g, kind, rows).wait_send()


def per_device(
    queries, keys, values, residual, w_out, neighbours, band_start, band_blocks, band_count
):
    tokens, width = queries.shape[1:]
    qblocks = band_count.shape[2]
    most = band_blocks.shape[3]
    cameras = lax.axis_size("cam")
    rigs = cameras // min(32, cameras)
    chunks = width // LANES
    cfg = (cameras, rigs, chunks, qblocks, most, width // HEADS)
    lanes = 2 if relays(cameras, rigs, qblocks) else 4
    dma = pltpu.SemaphoreType.DMA
    anywhere = pl.BlockSpec(memory_space=pl.ANY)
    scalars = pl.BlockSpec(memory_space=pltpu.SMEM)
    blocks = (qblocks, tokens // qblocks, width)
    attended = pl.pallas_call(
        functools.partial(kernel, cfg),
        out_shape=jax.ShapeDtypeStruct(blocks, jnp.bfloat16),
        in_specs=[anywhere] * 3 + [scalars] * 4,
        out_specs=pl.BlockSpec(memory_space=pltpu.VMEM),
        scratch_shapes=[pltpu.VMEM((2,) + blocks[:2] + (LANES,), jnp.bfloat16)] * (ROLES * chunks)
        + [pltpu.VMEM(blocks, jnp.bfloat16)] * 3
        + [
            dma((3,)),
            dma((lanes, chunks, max(2, qblocks))),
            dma((lanes, chunks, max(2, qblocks))),
            dma((2, chunks, qblocks)),
            dma((2, chunks, qblocks)),
        ],
        compiler_params=pltpu.CompilerParams(
            collective_id=0, has_side_effects=True, vmem_limit_bytes=62 * 1024 * 1024
        ),
        name="band_attention",
    )(*(x[0].reshape(blocks) for x in (queries, keys, values)), neighbours, band_start, band_blocks, band_count)
    result = residual[0].astype(jnp.float32) + jnp.dot(
        attended.reshape(tokens, width), w_out, preferred_element_type=jnp.float32
    )
    return result.astype(jnp.bfloat16)[None]


def solution(mesh):
    rows = ("scene", "cam")
    return jax.shard_map(
        per_device,
        mesh=mesh,
        in_specs=(
            P(rows, None, None),
            P(rows, None, None),
            P(rows, None, None),
            P(rows, None, None),
            P(),
            P(rows, None),
            P(rows, None),
            P(rows, None, None, None),
            P(rows, None, None),
        ),
        out_specs=P(rows, None, None),
        check_vma=False,
    )
```

profile of v0, /device:TPU:0, one launch (start us, length us, event | category | flops | bytes accessed | tf_op | source)
XLA Modules:
  0.0 96.3 jit_solution(17552824077744069526)
XLA Ops:
  0.0 1.4 %copy.10.block_ref = s32[1,4,6,2]{3,2,1,0:T(8,128)} copy(s32[1,4,6,2]{2,3,1,0:T(2,128)} %param.16) | data formatting | bytes 384 | tf_op args[7]
  1.4 0.0 copy-start
  1.4 89.9 %band_attention.1 = bf16[6,128,1024]{2,1,0:T(8,128)(2,1)} custom-call(bf16[6,128,1024]{2,1,0:T(8,128)(2,1)} %bitcast.13, bf16[6,128,1024]{2,1,0:T(8,128)(2,1)} %bitcast.14, bf16[6,128,1024]{2,1,0:T(8,128)(2,1)} %bitcast.15, s32[1,4]{1,0:T(1,128)} %near_ref.1, s32[1,4]{1,0:T(1,128)} %start_ref.1, s32[1,4,6,2]{3,2,1,0:T(8,128)} %copy.10.block_ref, ...), custom_call_target="tpu_custom_call" | custom-call | tf_op jit(solution)/shard_map/band_attention/pallas_call | solution.py:276
  91.3 0.0 copy-done
  91.3 5.0 %fusion.1 = bf16[1,768,1024]{2,1,0:T(8,128)(2,1)} fusion(bf16[768,1024]{1,0:T(8,128)(2,1)} %bitcast.16, bf16[1024,1024]{1,0:T(8,128)(2,1)} %param.13, bf16[1,768,1024]{2,1,0:T(8,128)(2,1)S(1)} %copy-done), kind=kOutput, calls=%fused_computation.2 | convolution fusion | flops 1612972032 | bytes 6815744 | tf_op jit(solution)/shard_map/dot_general | solution.py:295
Async XLA Ops:
  1.4 89.9 %copy-start = (bf16[1,768,1024]{2,1,0:T(8,128)(2,1)S(1)}, bf16[1,768,1024]{2,1,0:T(8,128)(2,1)}, u32[]{:S(2)}) copy-start(bf16[1,768,1024]{2,1,0:T(8,128)(2,1)} %param.12) | copy-start | bytes 4718596
where the time goes:
time: 96.5 us; the launch traced here: 96.3 us
  Pallas kernels  89.9 us (93%)
  matrix products  5.01 us (5%)
  local copies, waits for them, and re-layouts  1.39 us (1%)
    pallas_call x1, Pallas kernels, per_device(): pl.pallas_call(functools.partial(kernel, cfg), out_shape=jax.ShapeDtypeSt...  89.9 us
    dot_general x1, matrix products, per_device(): jnp.dot(attended.reshape(tokens, width), w_out, preferred_element_type=jn...  5.01 us

commit v1 on v0

v1 whole, which is shorter than its diff:
```python
import functools
import math

import jax
import jax.numpy as jnp
from jax import lax
from jax.experimental import pallas as pl
from jax.experimental.pallas import tpu as pltpu
from jax.sharding import PartitionSpec as P

HEADS = 16
LANES = 128
ROLES = 4
HIDDEN = -1e30
MESH = pl.DeviceIdType.MESH


def relays(cameras, rigs):
    return rigs == 1 and cameras % 4 == 0


def kernel(cfg, q_hbm, k_hbm, v_hbm, r_hbm, w_hbm, near_ref, start_ref, block_ref, count_ref, out_ref, *scratch):
    cameras, rigs, chunks, qblocks, most, head_dim = cfg
    relay = relays(cameras, rigs)
    take = iter(scratch)
    near = [[[next(take) for _ in range(chunks)] for _ in range(ROLES)] for _ in range(2)]
    q_ref, own_k, own_v, r_ref, w_ref, probs_ref, att_ref, acc_ref, own_sem = [next(take) for _ in range(9)]
    first_send, first_recv, x_send, z_send, b_send, b_recv, x_recv, z_recv = [next(take) for _ in range(8)]
    splits = x_recv.shape[2]
    size = near[0][0][0].shape[0] // splits
    own = (own_k, own_v)
    block_len = q_ref.shape[1]
    heads = LANES // head_dim
    pair = 2 if chunks % 2 == 0 else 1
    part_a, part_b, part_x, part_z = range(ROLES)
    me = lax.axis_index("cam")

    def at(offset):
        return lax.rem(me + offset + 2 * cameras, cameras)

    if relay:
        column = lax.rem(me // 2, 2)
        core = lax.rem(me, 2)
        partner = me + 1 - 2 * core
        across = me + 2 - 4 * column
        z_to = at(4 - 8 * column)
        z_from = at(8 * column - 4)
        from_x = lax.rem(column + core, 2) == 0
        z_view = at(4 * column - 2)
        partner_x = partner + 2 - 4 * column
        partner_z = lax.rem(partner + 4 * column - 2 + cameras, cameras)
        b_view = jnp.where(from_x, partner_z, partner_x)
        views = (partner, b_view, across, z_view)
        peers = (partner, across, z_to, z_from)
        first = ((part_a, partner),)
    else:
        views = (at(rigs), at(-rigs), at(2 * rigs), at(-2 * rigs))
        peers = views
        first = ((part_a, views[1]), (part_b, views[0]), (part_x, views[3]), (part_z, views[2]))

    loads = [
        pltpu.make_async_copy(src, dst, own_sem.at[n])
        for n, (src, dst) in enumerate(
            ((k_hbm, own_k), (v_hbm, own_v), (q_hbm, q_ref), (w_hbm, w_ref), (r_hbm, r_ref))
        )
    ]
    for copy in loads[:2]:
        copy.start()

    barrier = pltpu.get_barrier_semaphore()
    for peer in peers:
        pl.semaphore_signal(barrier, inc=1, device_id={"cam": peer}, device_id_type=MESH)
    pl.semaphore_wait(barrier, len(peers))

    def remote(src, dst, send, recv, target):
        return pltpu.make_async_remote_copy(
            src_ref=src, dst_ref=dst, send_sem=send, recv_sem=recv,
            device_id={"cam": target}, device_id_type=MESH,
        )

    def cols(g):
        return slice(g * LANES, (g + 1) * LANES)

    def some(part):
        return pl.ds(part * size, size)

    def first_copy(lane, g, kind):
        role, target = first[lane]
        return remote(
            own[kind].at[:, :, cols(g)], near[kind][role][g],
            first_send.at[lane, g, kind], first_recv.at[lane, g, kind], target,
        )

    def x_copy(g, kind, part):
        return remote(
            own[kind].at[some(part), :, cols(g)], near[kind][part_x][g].at[some(part)],
            x_send.at[g, kind], x_recv.at[g, kind, part], across,
        )

    def z_copy(g, kind, part):
        return remote(
            near[kind][part_x][g].at[some(part)], near[kind][part_z][g].at[some(part)],
            z_send.at[g, kind], z_recv.at[g, kind, part], z_to,
        )

    def b_copy(g, kind, part, source):
        return remote(
            near[kind][source][g].at[some(part)], near[kind][part_b][g].at[some(part)],
            b_send.at[g, kind], b_recv.at[g, kind], partner,
        )

    def whole(g, kind, send, recv):
        buffer = near[kind][part_b][g]
        return remote(buffer, buffer, send.at[g, kind], recv.at[g, kind], partner)

    def each(body, count=qblocks, unroll=1):
        def step(b, carry):
            body(b)
            return carry

        lax.fori_loop(0, count, step, 0, unroll=unroll)

    slots = []
    for view in views:
        slot = jnp.int32(0)
        for s in range(1, ROLES):
            slot = jnp.where(near_ref[0, s] == view, s, slot)
        slots.append(slot)
    starts = [start_ref[0, slot] for slot in slots]

    def listed(r, b, m):
        index = starts[r] + block_ref[0, slots[r], m, b]
        if m == 0:
            return index, None
        live = m < count_ref[0, slots[r], b]
        return jnp.where(live, index, 0), jnp.where(live, 0.0, HIDDEN)

    def score(g, b):
        q = q_ref[b, :, cols(g)] * jnp.asarray(1.0 / math.sqrt(head_dim), jnp.bfloat16)
        lane = lax.broadcasted_iota(jnp.int32, (block_len, LANES), 1) // head_dim
        q2 = jnp.concatenate([jnp.where(lane == h, q, jnp.zeros_like(q)) for h in range(heads)], axis=0)
        dims = (((1,), (1,)), ((), ()))

        def dot(keys):
            return lax.dot_general(q2, keys, dims, preferred_element_type=jnp.float32)

        scores = [dot(own_k[b, :, cols(g)])]
        for r in range(ROLES):
            found = [listed(r, b, m) for m in range(most)]
            got = dot(jnp.concatenate([near[0][r][g][index] for index, _ in found], axis=0))
            for m, (_, bias) in enumerate(found):
                piece = got[:, m * block_len:(m + 1) * block_len]
                scores.append(piece if bias is None else piece + bias)
        scores = jnp.concatenate(scores, axis=1)
        top = jnp.max(scores, axis=1, keepdims=True)
        expo = jnp.exp(scores - top)
        total = jnp.sum(expo, axis=1, keepdims=True)
        probs_ref[b] = (expo * (1.0 / total)).astype(jnp.bfloat16)

    def mix(g, b):
        lane = lax.broadcasted_iota(jnp.int32, (block_len, LANES), 1) // head_dim
        vals = [own_v[b, :, cols(g)]]
        for r in range(ROLES):
            vals += [near[1][r][g][listed(r, b, m)[0]] for m in range(most)]
        mixed = jnp.dot(probs_ref[b], jnp.concatenate(vals, axis=0), preferred_element_type=jnp.float32)
        result = mixed[:block_len]
        for h in range(1, heads):
            result = jnp.where(lane == h, mixed[h * block_len:(h + 1) * block_len], result)
        half = g % pair
        att_ref[b, :, half * LANES:(half + 1) * LANES] = result.astype(jnp.bfloat16)
        if half == pair - 1:
            rows = slice((g - half) * LANES, (g + 1) * LANES)
            base = r_ref[b].astype(jnp.float32) if g == half else acc_ref[b]
            summed = base + jnp.dot(att_ref[b], w_ref[rows, :], preferred_element_type=jnp.float32)
            if g == chunks - 1:
                out_ref[b] = summed.astype(out_ref.dtype)
            else:
                acc_ref[b] = summed

    for copy in loads[:2]:
        copy.wait()
    if relay:
        for g in range(chunks):
            for kind in range(2):
                each(lambda part: x_copy(g, kind, part).start(), splits)
    for copy in loads[2:]:
        copy.start()
    for lane in range(len(first)):
        for g in range(chunks):
            for kind in range(2):
                first_copy(lane, g, kind).start()

    def first_wait(g, kind):
        for lane in range(len(first)):
            first_copy(lane, g, kind).wait_recv()

    if relay:

        def after_x(g, kind, part):
            x_copy(g, kind, part).wait_recv()
            z_copy(g, kind, part).start()

            @pl.when(from_x)
            def _():
                b_copy(g, kind, part, part_x).start()

        def after_z(g, kind, part):
            z_copy(g, kind, part).wait_recv()

            @pl.when(jnp.logical_not(from_x))
            def _():
                b_copy(g, kind, part, part_z).start()

        def arrive(g, kind):
            first_wait(g, kind)
            whole(g, kind, b_send, b_recv).wait_recv()

        def drain(g, kind):
            for send in (x_send, z_send, b_send):
                whole(g, kind, send, b_recv).wait_send()

        for step in range(chunks + 2):
            if step == 1:
                for copy in loads[2:]:
                    copy.wait()
            for kind in range(2):
                work, done = (mix, step - 2) if kind == 0 else (score, step - 1)
                live = 0 <= done < chunks
                if live:
                    arrive(done, 1 - kind)
                if step > chunks:
                    if live:
                        each(lambda b: work(done, b), unroll=LAST if qblocks % LAST == 0 else 1)
                    continue

                def body(part):
                    if step < chunks:
                        after_x(step, kind, part)
                    if 1 <= step <= chunks:
                        after_z(step - 1, kind, part)
                    if live:
                        each(lambda b: work(done, part * size + b), size)

                each(body, splits)
                if 0 <= step - 3 < chunks - 2:
                    drain(step - 3, kind)

        for g in range(max(0, chunks - 2), chunks):
            for kind in range(2):
                drain(g, kind)
    else:
        for copy in loads[2:]:
            copy.wait()
        for g in range(chunks):
            first_wait(g, 0)
            each(lambda b: score(g, b))
            first_wait(g, 1)
            each(lambda b: mix(g, b))
    for lane in range(len(first)):
        for g in range(chunks):
            for kind in range(2):
                first_copy(lane, g, kind).wait_send()


def per_device(queries, keys, values, residual, w_out, neighbours, band_start, band_blocks, band_count):
    tokens, width = queries.shape[1:]
    qblocks = band_count.shape[2]
    most = band_blocks.shape[3]
    cameras = lax.axis_size("cam")
    rigs = cameras // min(32, cameras)
    chunks = width // LANES
    head_dim = width // HEADS
    cfg = (cameras, rigs, chunks, qblocks, most, head_dim)
    relay = relays(cameras, rigs)
    lanes = 1 if relay else ROLES
    dma = pltpu.SemaphoreType.DMA
    anywhere = pl.BlockSpec(memory_space=pltpu.HBM)
    scalars = pl.BlockSpec(memory_space=pltpu.SMEM)
    block_len = tokens // qblocks
    blocks = (qblocks, block_len, width)
    part = (qblocks, block_len, LANES)
    heads = LANES // head_dim
    pair = 2 if chunks % 2 == 0 else 1
    splits = math.gcd(SPLITS, qblocks)
    bf16 = jnp.bfloat16
    out = pl.pallas_call(
        functools.partial(kernel, cfg),
        out_shape=pltpu.VMEM(blocks, bf16),
        in_specs=[anywhere] * 5 + [scalars] * 4,
        out_specs=pl.BlockSpec(memory_space=pltpu.VMEM),
        scratch_shapes=[pltpu.VMEM(part, bf16)] * (2 * ROLES * chunks)
        + [pltpu.VMEM(blocks, bf16)] * 4
        + [
            pltpu.VMEM((width, width), bf16),
            pltpu.VMEM((qblocks, heads * block_len, (1 + ROLES * most) * block_len), bf16),
            pltpu.VMEM((qblocks, block_len, pair * LANES), bf16),
            pltpu.VMEM(blocks, jnp.float32),
            dma((5,)),
            dma((lanes, chunks, 2)),
            dma((lanes, chunks, 2)),
        ]
        + [dma((chunks, 2) if relay else (1, 1))] * 4
        + [dma((chunks, 2, splits) if relay else (1, 1, 1))] * 2,
        compiler_params=pltpu.CompilerParams(
            collective_id=0, has_side_effects=True, vmem_limit_bytes=VMEM_LIMIT * 1024 * 1024
        ),
        name="band_attention",
    )(
        *(x[0].reshape(blocks) for x in (queries, keys, values, residual)),
        w_out, neighbours, band_start, jnp.swapaxes(band_blocks, 2, 3), band_count,
    )
    return out.reshape(tokens, width)[None]


VMEM_LIMIT = 62
SPLITS = 3
LAST = 3


def solution(mesh):
    rows = ("scene", "cam")
    return jax.shard_map(
        per_device,
        mesh=mesh,
        in_specs=(
            P(rows, None, None),
            P(rows, None, None),
            P(rows, None, None),
            P(rows, None, None),
            P(),
            P(rows, None),
            P(rows, None),
            P(rows, None, None, None),
            P(rows, None, None),
        ),
        out_specs=P(rows, None, None),
        check_vma=False,
    )
```

time: 96.5 us -> 88.4 us (0.916)
  matrix products: 5.01 us -> 0 us
  Pallas kernels: 89.9 us -> 87.1 us
    dot_general x1 -> x0, matrix products: 5.01 us -> none  [per_device(): jnp.dot(attended.reshape(tokens, width), w_out, preferred_element_type=jn...]
    pallas_call x1, Pallas kernels: 89.9 us -> 87.1 us  [per_device(): pl.pallas_call(functools.partial(kernel, cfg), out_shape=pltpu.VMEM(block...]
where the time goes in v1:
time: 88.4 us; the launch traced here: 88.2 us
  Pallas kernels  87.1 us (99%)
  local copies, waits for them, and re-layouts  1.15 us (1%)
    pallas_call x1, Pallas kernels, per_device(): pl.pallas_call(functools.partial(kernel, cfg), out_shape=pltpu.VMEM(block...  87.1 us

profile of v1, /device:TPU:0, one launch (start us, length us, event | category | flops | bytes accessed | tf_op | source)
XLA Modules:
  0.0 88.2 jit_solution(13737273509184586270)
XLA Ops:
  0.0 87.1 %band_attention.1 = bf16[6,128,1024]{2,1,0:T(8,128)(2,1)S(1)} custom-call(bf16[6,128,1024]{2,1,0:T(8,128)(2,1)} %bitcast.7, bf16[6,128,1024]{2,1,0:T(8,128)(2,1)} %bitcast.8, bf16[6,128,1024]{2,1,0:T(8,128)(2,1)} %bitcast.9, bf16[6,128,1024]{2,1,0:T(8,128)(2,1)} %bitcast.10, bf16[1024,1024]{1,0:T(8,128)(2,1)} %w_hbm.1, s32[1,4]{1,0:T(1,128)} %near_ref.1, ...), custom_call_target="tpu_custom_call" | custom-call | tf_op jit(solution)/shard_map/band_attention/pallas_call | solution.py:286
  87.1 1.1 %copy.11 = bf16[1,768,1024]{2,1,0:T(8,128)(2,1)} copy(bf16[1,768,1024]{2,1,0:T(8,128)(2,1)S(1)} %bitcast.6) | data formatting | bytes 3145728

commit v2 on v1

--- a/solution.py
+++ b/solution.py
@@ -11,28 +11,44 @@
 HEADS = 16
 LANES = 128
 ROLES = 4
+WIN = 3
 HIDDEN = -1e30
 MESH = pl.DeviceIdType.MESH
 
 
 def relays(cameras, rigs):
     return rigs == 1 and cameras % 4 == 0
+
+
+def cuts(cfg, role, g, kind):
+    cameras, rigs, chunks = cfg[:3]
+    if role != 2 or not relays(cameras, rigs) or g < chunks - 1:
+        return 1
+    return CUTS[kind]
 
 
 def kernel(cfg, q_hbm, k_hbm, v_hbm, r_hbm, w_hbm, near_ref, start_ref, block_ref, count_ref, out_ref, *scratch):
     cameras, rigs, chunks, qblocks, most, head_dim = cfg
     relay = relays(cameras, rigs)
     take = iter(scratch)
-    near = [[[next(take) for _ in range(chunks)] for _ in range(ROLES)] for _ in range(2)]
+    part_a, part_b, part_x, part_z = range(ROLES)
+    near = [
+        [[[next(take) for _ in range(cuts(cfg, role, g, kind))] for g in range(chunks)] for role in range(ROLES)]
+        for kind in range(2)
+    ]
     q_ref, own_k, own_v, r_ref, w_ref, probs_ref, att_ref, acc_ref, own_sem = [next(take) for _ in range(9)]
-    first_send, first_recv, x_send, z_send, b_send, b_recv, x_recv, z_recv = [next(take) for _ in range(8)]
-    splits = x_recv.shape[2]
-    size = near[0][0][0].shape[0] // splits
+    first_send, first_recv = next(take), next(take)
+    if relay:
+        near_sem, far_sem, told_near, told_start, tell_send, tell_recv = [next(take) for _ in range(6)]
+        x_send, z_send, b_send, z_recv, b_recv, x_recv = [next(take) for _ in range(6)]
+        staged = [
+            [[[next(take) for _ in range(2)] for _ in range(cuts(cfg, part_x, g, kind))] for g in range(chunks)]
+            for kind in range(2)
+        ]
     own = (own_k, own_v)
     block_len = q_ref.shape[1]
     heads = LANES // head_dim
     pair = 2 if chunks % 2 == 0 else 1
-    part_a, part_b, part_x, part_z = range(ROLES)
     me = lax.axis_index("cam")
 
     def at(offset):
@@ -51,11 +67,9 @@
         partner_z = lax.rem(partner + 4 * column - 2 + cameras, cameras)
         b_view = jnp.where(from_x, partner_z, partner_x)
         views = (partner, b_view, across, z_view)
-        peers = (partner, across, z_to, z_from)
         first = ((part_a, partner),)
     else:
         views = (at(rigs), at(-rigs), at(2 * rigs), at(-2 * rigs))
-        peers = views
         first = ((part_a, views[1]), (part_b, views[0]), (part_x, views[3]), (part_z, views[2]))
 
     loads = [
@@ -67,10 +81,31 @@
     for copy in loads[:2]:
         copy.start()
 
+    def signal(sem, peer):
+        pl.semaphore_signal(sem, inc=1, device_id={"cam": peer}, device_id_type=MESH)
+
     barrier = pltpu.get_barrier_semaphore()
-    for peer in peers:
-        pl.semaphore_signal(barrier, inc=1, device_id={"cam": peer}, device_id_type=MESH)
-    pl.semaphore_wait(barrier, len(peers))
+    if relay:
+        signal(barrier, across - core)
+        signal(barrier, z_from + 1 - core)
+        signal(barrier, z_to + 1 - core)
+
+        @pl.when(core == 1)
+        def _():
+            signal(barrier, partner)
+
+        @pl.when(core == 0)
+        def _():
+            pl.semaphore_wait(barrier, 3)
+            signal(near_sem, partner)
+
+        @pl.when(core == 1)
+        def _():
+            pl.semaphore_wait(near_sem, 1)
+    else:
+        for view in views:
+            signal(barrier, view)
+        pl.semaphore_wait(barrier, len(views))
 
     def remote(src, dst, send, recv, target):
         return pltpu.make_async_remote_copy(
@@ -81,36 +116,44 @@
     def cols(g):
         return slice(g * LANES, (g + 1) * LANES)
 
-    def some(part):
-        return pl.ds(part * size, size)
-
     def first_copy(lane, g, kind):
         role, target = first[lane]
         return remote(
-            own[kind].at[:, :, cols(g)], near[kind][role][g],
+            own[kind].at[:, :, cols(g)], near[kind][role][g][0],
             first_send.at[lane, g, kind], first_recv.at[lane, g, kind], target,
         )
 
+    def rows(g, kind, part):
+        size = block_len // cuts(cfg, part_x, g, kind)
+        return pl.ds(part * size, size)
+
     def x_copy(g, kind, part):
+        source = own if g else (k_hbm, v_hbm)
         return remote(
-            own[kind].at[some(part), :, cols(g)], near[kind][part_x][g].at[some(part)],
+            source[kind].at[:, rows(g, kind, part), cols(g)], near[kind][part_x][g][part],
             x_send.at[g, kind], x_recv.at[g, kind, part], across,
         )
 
     def z_copy(g, kind, part):
         return remote(
-            near[kind][part_x][g].at[some(part)], near[kind][part_z][g].at[some(part)],
-            z_send.at[g, kind], z_recv.at[g, kind, part], z_to,
-        )
-
-    def b_copy(g, kind, part, source):
+            staged[kind][g][part][0], near[kind][part_z][g][0].at[:, rows(g, kind, part)],
+            z_send.at[g, kind], z_recv.at[g, kind], z_to,
+        )
+
+    def far_copy(g, kind, part):
         return remote(
-            near[kind][source][g].at[some(part)], near[kind][part_b][g].at[some(part)],
+            staged[kind][g][part][1], near[kind][part_b][g][0].at[pl.ds(0, WIN), rows(g, kind, part)],
+            b_send.at[g, kind], b_recv.at[g, kind], z_to + 1 - 2 * core,
+        )
+
+    def near_copy(g, kind, part):
+        return remote(
+            near[kind][part_x][g][part], near[kind][part_b][g][0].at[:, rows(g, kind, part)],
             b_send.at[g, kind], b_recv.at[g, kind], partner,
         )
 
-    def whole(g, kind, send, recv):
-        buffer = near[kind][part_b][g]
+    def whole(g, kind, role, send, recv):
+        buffer = near[kind][role][g][0]
         return remote(buffer, buffer, send.at[g, kind], recv.at[g, kind], partner)
 
     def each(body, count=qblocks, unroll=1):
@@ -127,6 +170,9 @@
             slot = jnp.where(near_ref[0, s] == view, s, slot)
         slots.append(slot)
     starts = [start_ref[0, slot] for slot in slots]
+    if relay:
+        starts[part_z] = jnp.int32(0)
+        starts[part_b] = jnp.where(from_x, 0, starts[part_b])
 
     def listed(r, b, m):
         index = starts[r] + block_ref[0, slots[r], m, b]
@@ -147,7 +193,7 @@
         scores = [dot(own_k[b, :, cols(g)])]
         for r in range(ROLES):
             found = [listed(r, b, m) for m in range(most)]
-            got = dot(jnp.concatenate([near[0][r][g][index] for index, _ in found], axis=0))
+            got = dot(jnp.concatenate([part[index] for index, _ in found for part in near[0][r][g]], axis=0))
             for m, (_, bias) in enumerate(found):
                 piece = got[:, m * block_len:(m + 1) * block_len]
                 scores.append(piece if bias is None else piece + bias)
@@ -161,7 +207,7 @@
         lane = lax.broadcasted_iota(jnp.int32, (block_len, LANES), 1) // head_dim
         vals = [own_v[b, :, cols(g)]]
         for r in range(ROLES):
-            vals += [near[1][r][g][listed(r, b, m)[0]] for m in range(most)]
+            vals += [part[listed(r, b, m)[0]] for m in range(most) for part in near[1][r][g]]
         mixed = jnp.dot(probs_ref[b], jnp.concatenate(vals, axis=0), preferred_element_type=jnp.float32)
         result = mixed[:block_len]
         for h in range(1, heads):
@@ -177,12 +223,17 @@
             else:
                 acc_ref[b] = summed
 
+    parts = [(g, kind, part) for g in range(chunks) for kind in range(2) for part in range(cuts(cfg, part_x, g, kind))]
+    if relay:
+        for g, kind, part in parts:
+            if g == 0:
+                x_copy(g, kind, part).start()
     for copy in loads[:2]:
         copy.wait()
     if relay:
-        for g in range(chunks):
-            for kind in range(2):
-                each(lambda part: x_copy(g, kind, part).start(), splits)
+        for g, kind, part in parts:
+            if g > 0:
+                x_copy(g, kind, part).start()
     for copy in loads[2:]:
         copy.start()
     for lane in range(len(first)):
@@ -196,56 +247,108 @@
 
     if relay:
 
-        def after_x(g, kind, part):
+        @pl.when(core == 1)
+        def _():
+            pl.semaphore_wait(barrier, 4)
+            signal(far_sem, partner)
+
+        @pl.when(core == 0)
+        def _():
+            pl.semaphore_wait(far_sem, 1)
+
+        def tell(n, k):
+            row, place = ((near_ref, told_near), (start_ref, told_start))[k]
+            return remote(row, place.at[core], tell_send.at[n, k], tell_recv.at[core, k], z_from - core + n)
+
+        def told(n, view):
+            start = told_start[n, 0, 0]
+            for s in range(1, ROLES):
+                start = jnp.where(told_near[n, 0, s] == view, told_start[n, 0, s], start)
+            return start
+
+        for n in range(2):
+            for k in range(2):
+                tell(n, k).start()
+        for n in range(2):
+            for k in range(2):
+                tell(n, k).wait_send()
+        for n in range(2):
+            for k in range(2):
+                remote(
+                    told_near.at[n], (told_near, told_start)[k].at[n], tell_send.at[n, k], tell_recv.at[n, k], partner
+                ).wait_recv()
+        start_z = told(core, across)
+        start_b = told(1 - core, across)
+
+        def relay_part(g, kind, part):
             x_copy(g, kind, part).wait_recv()
+            source = near[kind][part_x][g][part]
+            for n in range(WIN):
+                staged[kind][g][part][0][n] = source[start_z + n]
             z_copy(g, kind, part).start()
 
             @pl.when(from_x)
             def _():
-                b_copy(g, kind, part, part_x).start()
-
-        def after_z(g, kind, part):
-            z_copy(g, kind, part).wait_recv()
+                near_copy(g, kind, part).start()
 
             @pl.when(jnp.logical_not(from_x))
             def _():
-                b_copy(g, kind, part, part_z).start()
+                for n in range(WIN):
+                    staged[kind][g][part][1][n] = source[start_b + n]
+                far_copy(g, kind, part).start()
 
         def arrive(g, kind):
             first_wait(g, kind)
-            whole(g, kind, b_send, b_recv).wait_recv()
+
+            @pl.when(from_x)
+            def _():
+                whole(g, kind, part_z, b_send, b_recv).wait_recv()
+
+            @pl.when(jnp.logical_not(from_x))
+            def _():
+                whole(g, kind, part_b, b_send, b_recv).wait_recv()
+
+            whole(g, kind, part_z, z_send, z_recv).wait_recv()
 
         def drain(g, kind):
-            for send in (x_send, z_send, b_send):
-                whole(g, kind, send, b_recv).wait_send()
-
-        for step in range(chunks + 2):
-            if step == 1:
+            whole(g, kind, part_b, x_send, b_recv).wait_send()
+            whole(g, kind, part_z, z_send, b_recv).wait_send()
+
+            @pl.when(from_x)
+            def _():
+                whole(g, kind, part_b, b_send, b_recv).wait_send()
+
+            @pl.when(jnp.logical_not(from_x))
+            def _():
+                whole(g, kind, part_z, b_send, b_recv).wait_send()
+
+        def run(work, g, kind, low, high, unroll=2):
+            if low == 0:
+                arrive(g, kind)
+            count = high - low
+            each(lambda b: work(g, low + b), count, unroll if count % unroll == 0 else 1)
+
+        end = chunks - 1
+        for g, kind, part in parts:
+            relay_part(g, kind, part)
+            if g == 1 and kind == 0 and part == 0:
                 for copy in loads[2:]:
                     copy.wait()
-            for kind in range(2):
-                work, done = (mix, step - 2) if kind == 0 else (score, step - 1)
-                live = 0 <= done < chunks
-                if live:
-                    arrive(done, 1 - kind)
-                if step > chunks:
-                    if live:
-                        each(lambda b: work(done, b), unroll=LAST if qblocks % LAST == 0 else 1)
-                    continue
-
-                def body(part):
-                    if step < chunks:
-                        after_x(step, kind, part)
-                    if 1 <= step <= chunks:
-                        after_z(step - 1, kind, part)
-                    if live:
-                        each(lambda b: work(done, part * size + b), size)
-
-                each(body, splits)
-                if 0 <= step - 3 < chunks - 2:
-                    drain(step - 3, kind)
-
-        for g in range(max(0, chunks - 2), chunks):
+            if g == 0:
+                continue
+            if g < end:
+                run((score, mix)[kind], g - 1, kind, 0, qblocks)
+                if g >= 2:
+                    drain(g - 2, kind)
+            elif kind == 0:
+                n = cuts(cfg, part_x, g, kind)
+                run(score, g - 1, 0, part * qblocks // n, (part + 1) * qblocks // n, 3)
+            elif part >= cuts(cfg, part_x, g, kind) - 2:
+                n = part - cuts(cfg, part_x, g, kind) + 2
+                run(mix, g - 1, 1, n * qblocks // 2, (n + 1) * qblocks // 2, 3)
+        run(score, end, 0, 0, qblocks)
+        run(mix, end, 1, 0, qblocks, LAST)
+        for g in range(max(0, end - 2), chunks):
             for kind in range(2):
                 drain(g, kind)
     else:
@@ -253,9 +356,9 @@
             copy.wait()
         for g in range(chunks):
             first_wait(g, 0)
-            each(lambda b: score(g, b))
+            each(lambda b: score(g, b), qblocks)
             first_wait(g, 1)
-            each(lambda b: mix(g, b))
+            each(lambda b: mix(g, b), qblocks)
     for lane in range(len(first)):
         for g in range(chunks):
             for kind in range(2):
@@ -278,29 +381,39 @@
     scalars = pl.BlockSpec(memory_space=pltpu.SMEM)
     block_len = tokens // qblocks
     blocks = (qblocks, block_len, width)
-    part = (qblocks, block_len, LANES)
     heads = LANES // head_dim
     pair = 2 if chunks % 2 == 0 else 1
-    splits = math.gcd(SPLITS, qblocks)
     bf16 = jnp.bfloat16
+    regular = pltpu.SemaphoreType.REGULAR
+    scratch = []
+    for kind in range(2):
+        for role in range(ROLES):
+            for g in range(chunks):
+                n = cuts(cfg, role, g, kind)
+                count = WIN if relay and role == 3 else qblocks
+                scratch += [pltpu.VMEM((count, block_len // n, LANES), bf16)] * n
+    scratch += [pltpu.VMEM(blocks, bf16)] * 4 + [
+        pltpu.VMEM((width, width), bf16),
+        pltpu.VMEM((qblocks, heads * block_len, (1 + ROLES * most) * block_len), bf16),
+        pltpu.VMEM((qblocks, block_len, pair * LANES), bf16),
+        pltpu.VMEM(blocks, jnp.float32),
+        dma((5,)),
+        dma((lanes, chunks, 2)),
+        dma((lanes, chunks, 2)),
+    ]
+    if relay:
+        scratch += [regular, regular, pltpu.SMEM((2, 1, ROLES), jnp.int32), pltpu.SMEM((2, 1, ROLES), jnp.int32), dma((2, 2)), dma((2, 2))]
+        scratch += [dma((chunks, 2))] * 5 + [dma((chunks, 2, max(CUTS)))]
+        for kind in range(2):
+            for g in range(chunks):
+                n = cuts(cfg, 2, g, kind)
+                scratch += [pltpu.VMEM((WIN, block_len // n, LANES), bf16)] * (2 * n)
     out = pl.pallas_call(
         functools.partial(kernel, cfg),
         out_shape=pltpu.VMEM(blocks, bf16),
         in_specs=[anywhere] * 5 + [scalars] * 4,
         out_specs=pl.BlockSpec(memory_space=pltpu.VMEM),
-        scratch_shapes=[pltpu.VMEM(part, bf16)] * (2 * ROLES * chunks)
-        + [pltpu.VMEM(blocks, bf16)] * 4
-        + [
-            pltpu.VMEM((width, width), bf16),
-            pltpu.VMEM((qblocks, heads * block_len, (1 + ROLES * most) * block_len), bf16),
-            pltpu.VMEM((qblocks, block_len, pair * LANES), bf16),
-            pltpu.VMEM(blocks, jnp.float32),
-            dma((5,)),
-            dma((lanes, chunks, 2)),
-            dma((lanes, chunks, 2)),
-        ]
-        + [dma((chunks, 2) if relay else (1, 1))] * 4
-        + [dma((chunks, 2, splits) if relay else (1, 1, 1))] * 2,
+        scratch_shapes=scratch,
         compiler_params=pltpu.CompilerParams(
             collective_id=0, has_side_effects=True, vmem_limit_bytes=VMEM_LIMIT * 1024 * 1024
         ),
@@ -313,7 +426,7 @@
 
 
 VMEM_LIMIT = 62
-SPLITS = 3
+CUTS = (2, 4)
 LAST = 3
 
 

time: 88.4 us -> 84.3 us (0.954)
  Pallas kernels: 87.1 us -> 83 us
    pallas_call x1, Pallas kernels: 87.1 us -> 83 us  [per_device(): pl.pallas_call(functools.partial(kernel, cfg), out_shape=pltpu.VMEM(block...]
where the time goes in v2:
time: 84.3 us; the launch traced here: 84.1 us
  Pallas kernels  83 us (98%)
  local copies, waits for them, and re-layouts  1.15 us (1%)
    pallas_call x1, Pallas kernels, per_device(): pl.pallas_call(functools.partial(kernel, cfg), out_shape=pltpu.VMEM(block...  83 us

profile of v2, /device:TPU:0, one launch (start us, length us, event | category | flops | bytes accessed | tf_op | source)
XLA Modules:
  0.0 84.1 jit_solution(5828749402543543715)
XLA Ops:
  0.0 83.0 %band_attention.1 = bf16[6,128,1024]{2,1,0:T(8,128)(2,1)S(1)} custom-call(bf16[6,128,1024]{2,1,0:T(8,128)(2,1)} %bitcast.7, bf16[6,128,1024]{2,1,0:T(8,128)(2,1)} %bitcast.8, bf16[6,128,1024]{2,1,0:T(8,128)(2,1)} %bitcast.9, bf16[6,128,1024]{2,1,0:T(8,128)(2,1)} %bitcast.10, bf16[1024,1024]{1,0:T(8,128)(2,1)} %w_hbm.1, s32[1,4]{1,0:T(1,128)} %near_ref.1, ...), custom_call_target="tpu_custom_call" | custom-call | tf_op jit(solution)/shard_map/band_attention/pallas_call | solution.py:411
  83.0 1.1 %copy.11 = bf16[1,768,1024]{2,1,0:T(8,128)(2,1)} copy(bf16[1,768,1024]{2,1,0:T(8,128)(2,1)S(1)} %bitcast.6) | data formatting | bytes 3145728

commit v3 on v2

--- a/solution.py
+++ b/solution.py
@@ -12,6 +12,7 @@
 LANES = 128
 ROLES = 4
 WIN = 3
+X_ROLE = 1
 HIDDEN = -1e30
 MESH = pl.DeviceIdType.MESH
 
@@ -22,8 +23,8 @@
 
 def cuts(cfg, role, g, kind):
     cameras, rigs, chunks = cfg[:3]
-    if role != 2 or not relays(cameras, rigs) or g < chunks - 1:
-        return 1
+    if role != X_ROLE or not relays(cameras, rigs) or g < chunks - 1:
+        return (1,)
     return CUTS[kind]
 
 
@@ -31,18 +32,18 @@
     cameras, rigs, chunks, qblocks, most, head_dim = cfg
     relay = relays(cameras, rigs)
     take = iter(scratch)
-    part_a, part_b, part_x, part_z = range(ROLES)
+    part_a, part_x, part_b, part_z = range(ROLES)
     near = [
-        [[[next(take) for _ in range(cuts(cfg, role, g, kind))] for g in range(chunks)] for role in range(ROLES)]
+        [[[next(take) for _ in cuts(cfg, role, g, kind)] for g in range(chunks)] for role in range(ROLES)]
         for kind in range(2)
     ]
     q_ref, own_k, own_v, r_ref, w_ref, probs_ref, att_ref, acc_ref, own_sem = [next(take) for _ in range(9)]
     first_send, first_recv = next(take), next(take)
     if relay:
-        near_sem, far_sem, told_near, told_start, tell_send, tell_recv = [next(take) for _ in range(6)]
+        mixed_ref, near_sem, far_sem, told_near, told_start, tell_send, tell_recv = [next(take) for _ in range(7)]
         x_send, z_send, b_send, z_recv, b_recv, x_recv = [next(take) for _ in range(6)]
         staged = [
-            [[[next(take) for _ in range(2)] for _ in range(cuts(cfg, part_x, g, kind))] for g in range(chunks)]
+            [[[next(take) for _ in range(2)] for _ in cuts(cfg, part_x, g, kind)] for g in range(chunks)]
             for kind in range(2)
         ]
     own = (own_k, own_v)
@@ -66,11 +67,11 @@
         partner_x = partner + 2 - 4 * column
         partner_z = lax.rem(partner + 4 * column - 2 + cameras, cameras)
         b_view = jnp.where(from_x, partner_z, partner_x)
-        views = (partner, b_view, across, z_view)
+        views = (partner, across, b_view, z_view)
         first = ((part_a, partner),)
     else:
         views = (at(rigs), at(-rigs), at(2 * rigs), at(-2 * rigs))
-        first = ((part_a, views[1]), (part_b, views[0]), (part_x, views[3]), (part_z, views[2]))
+        first = ((0, views[1]), (1, views[0]), (2, views[3]), (3, views[2]))
 
     loads = [
         pltpu.make_async_copy(src, dst, own_sem.at[n])
@@ -124,8 +125,8 @@
         )
 
     def rows(g, kind, part):
-        size = block_len // cuts(cfg, part_x, g, kind)
-        return pl.ds(part * size, size)
+        sizes = [block_len // n for n in cuts(cfg, part_x, g, kind)]
+        return pl.ds(sum(sizes[:part]), sizes[part])
 
     def x_copy(g, kind, part):
         source = own if g else (k_hbm, v_hbm)
@@ -203,27 +204,56 @@
         total = jnp.sum(expo, axis=1, keepdims=True)
         probs_ref[b] = (expo * (1.0 / total)).astype(jnp.bfloat16)
 
+    def weigh(g, b, roles):
+        vals = []
+        for r in roles:
+            if r < 0:
+                vals.append(own_v[b, :, cols(g)])
+            else:
+                vals += [part[listed(r, b, m)[0]] for m in range(most) for part in near[1][r][g]]
+        low = 0 if roles[0] < 0 else (1 + roles[0] * most) * block_len
+        high = (1 + (roles[-1] + 1) * most) * block_len
+        return jnp.dot(probs_ref[b, :, low:high], jnp.concatenate(vals, axis=0), preferred_element_type=jnp.float32)
+
+    def early(g, b):
+        mixed_ref[b] = weigh(g, b, (-1, part_a, part_x))
+
+    def late(g, b):
+        finish(g, b, mixed_ref[b] + weigh(g, b, (part_b, part_z)))
+
     def mix(g, b):
+        finish(g, b, weigh(g, b, tuple(range(-1, ROLES))))
+
+    def finish(g, b, mixed):
         lane = lax.broadcasted_iota(jnp.int32, (block_len, LANES), 1) // head_dim
-        vals = [own_v[b, :, cols(g)]]
-        for r in range(ROLES):
-            vals += [part[listed(r, b, m)[0]] for m in range(most) for part in near[1][r][g]]
-        mixed = jnp.dot(probs_ref[b], jnp.concatenate(vals, axis=0), preferred_element_type=jnp.float32)
         result = mixed[:block_len]
         for h in range(1, heads):
             result = jnp.where(lane == h, mixed[h * block_len:(h + 1) * block_len], result)
         half = g % pair
-        att_ref[b, :, half * LANES:(half + 1) * LANES] = result.astype(jnp.bfloat16)
-        if half == pair - 1:
-            rows = slice((g - half) * LANES, (g + 1) * LANES)
+        place = pl.ds(pl.multiple_of(b * block_len, block_len), block_len)
+        att_ref[place, half * LANES:(half + 1) * LANES] = result.astype(jnp.bfloat16)
+
+    def project(g, group, count):
+        half = g % pair
+        if half < pair - 1:
+            return
+        place = pl.ds(pl.multiple_of(group * count * block_len, block_len), count * block_len)
+        rows = slice((g - half) * LANES, (g + 1) * LANES)
+        added = jnp.dot(att_ref[place, :], w_ref[rows, :], preferred_element_type=jnp.float32)
+        for n in range(count):
+            b = group * count + n
             base = r_ref[b].astype(jnp.float32) if g == half else acc_ref[b]
-            summed = base + jnp.dot(att_ref[b], w_ref[rows, :], preferred_element_type=jnp.float32)
+            summed = base + added[n * block_len:(n + 1) * block_len]
             if g == chunks - 1:
                 out_ref[b] = summed.astype(out_ref.dtype)
             else:
                 acc_ref[b] = summed
 
-    parts = [(g, kind, part) for g in range(chunks) for kind in range(2) for part in range(cuts(cfg, part_x, g, kind))]
+    def project_all(g):
+        count = GROUP if qblocks % GROUP == 0 else 1
+        each(lambda group: project(g, group, count), qblocks // count)
+
+    parts = [(g, kind, part) for g in range(chunks) for kind in range(2) for part in range(len(cuts(cfg, part_x, g, kind)))]
     if relay:
         for g, kind, part in parts:
             if g == 0:
@@ -297,8 +327,9 @@
                     staged[kind][g][part][1][n] = source[start_b + n]
                 far_copy(g, kind, part).start()
 
-        def arrive(g, kind):
-            first_wait(g, kind)
+        def arrive(g, kind, all_roles=True):
+            if all_roles:
+                first_wait(g, kind)
 
             @pl.when(from_x)
             def _():
@@ -327,6 +358,8 @@
                 arrive(g, kind)
             count = high - low
             each(lambda b: work(g, low + b), count, unroll if count % unroll == 0 else 1)
+            if work is mix and high == qblocks:
+                project_all(g)
 
         end = chunks - 1
         for g, kind, part in parts:
@@ -341,13 +374,23 @@
                 if g >= 2:
                     drain(g - 2, kind)
             elif kind == 0:
-                n = cuts(cfg, part_x, g, kind)
+                n = len(cuts(cfg, part_x, g, kind))
                 run(score, g - 1, 0, part * qblocks // n, (part + 1) * qblocks // n, 3)
-            elif part >= cuts(cfg, part_x, g, kind) - 2:
-                n = part - cuts(cfg, part_x, g, kind) + 2
+            elif part >= len(cuts(cfg, part_x, g, kind)) - 2:
+                n = part - len(cuts(cfg, part_x, g, kind)) + 2
                 run(mix, g - 1, 1, n * qblocks // 2, (n + 1) * qblocks // 2, 3)
         run(score, end, 0, 0, qblocks)
-        run(mix, end, 1, 0, qblocks, LAST)
+        first_wait(end, 1)
+        each(lambda b: early(end, b), qblocks, LAST)
+        arrive(end, 1, False)
+        count = TAIL if qblocks % TAIL == 0 else 1
+
+        def close(group):
+            for n in range(count):
+                late(end, group * count + n)
+            project(end, group, count)
+
+        each(close, qblocks // count, TAIL_UNROLL)
         for g in range(max(0, end - 2), chunks):
             for kind in range(2):
                 drain(g, kind)
@@ -359,6 +402,7 @@
             each(lambda b: score(g, b), qblocks)
             first_wait(g, 1)
             each(lambda b: mix(g, b), qblocks)
+            project_all(g)
     for lane in range(len(first)):
         for g in range(chunks):
             for kind in range(2):
@@ -389,25 +433,24 @@
     for kind in range(2):
         for role in range(ROLES):
             for g in range(chunks):
-                n = cuts(cfg, role, g, kind)
-                count = WIN if relay and role == 3 else qblocks
-                scratch += [pltpu.VMEM((count, block_len // n, LANES), bf16)] * n
+                count = WIN if relay and role == ROLES - 1 else qblocks
+                scratch += [pltpu.VMEM((count, block_len // n, LANES), bf16) for n in cuts(cfg, role, g, kind)]
     scratch += [pltpu.VMEM(blocks, bf16)] * 4 + [
         pltpu.VMEM((width, width), bf16),
         pltpu.VMEM((qblocks, heads * block_len, (1 + ROLES * most) * block_len), bf16),
-        pltpu.VMEM((qblocks, block_len, pair * LANES), bf16),
+        pltpu.VMEM((qblocks * block_len, pair * LANES), bf16),
         pltpu.VMEM(blocks, jnp.float32),
         dma((5,)),
         dma((lanes, chunks, 2)),
         dma((lanes, chunks, 2)),
     ]
     if relay:
-        scratch += [regular, regular, pltpu.SMEM((2, 1, ROLES), jnp.int32), pltpu.SMEM((2, 1, ROLES), jnp.int32), dma((2, 2)), dma((2, 2))]
-        scratch += [dma((chunks, 2))] * 5 + [dma((chunks, 2, max(CUTS)))]
+        scratch += [pltpu.VMEM((qblocks, heads * block_len, LANES), jnp.float32), regular, regular, pltpu.SMEM((2, 1, ROLES), jnp.int32), pltpu.SMEM((2, 1, ROLES), jnp.int32), dma((2, 2)), dma((2, 2))]
+        scratch += [dma((chunks, 2))] * 5 + [dma((chunks, 2, max(len(c) for c in CUTS)))]
         for kind in range(2):
             for g in range(chunks):
-                n = cuts(cfg, 2, g, kind)
-                scratch += [pltpu.VMEM((WIN, block_len // n, LANES), bf16)] * (2 * n)
+                for n in cuts(cfg, X_ROLE, g, kind):
+                    scratch += [pltpu.VMEM((WIN, block_len // n, LANES), bf16)] * 2
     out = pl.pallas_call(
         functools.partial(kernel, cfg),
         out_shape=pltpu.VMEM(blocks, bf16),
@@ -426,8 +469,11 @@
 
 
 VMEM_LIMIT = 62
-CUTS = (2, 4)
-LAST = 3
+CUTS = ((2, 2), (2, 4, 8, 8))
+LAST = 6
+GROUP = 3
+TAIL = 6
+TAIL_UNROLL = 1
 
 
 def solution(mesh):

time: 84.3 us -> 82.9 us (0.983)
  Pallas kernels: 83 us -> 81.6 us
    pallas_call x1, Pallas kernels: 83 us -> 81.6 us  [per_device(): pl.pallas_call(functools.partial(kernel, cfg), out_shape=pltpu.VMEM(block...]
where the time goes in v3:
time: 82.9 us; the launch traced here: 82.8 us
  Pallas kernels  81.6 us (98%)
  local copies, waits for them, and re-layouts  1.15 us (1%)
    pallas_call x1, Pallas kernels, per_device(): pl.pallas_call(functools.partial(kernel, cfg), out_shape=pltpu.VMEM(block...  81.6 us

profile of v3, /device:TPU:0, one launch (start us, length us, event | category | flops | bytes accessed | tf_op | source)
XLA Modules:
  0.0 82.8 jit_solution(8977640107902114400)
XLA Ops:
  0.0 81.6 %band_attention.1 = bf16[6,128,1024]{2,1,0:T(8,128)(2,1)S(1)} custom-call(bf16[6,128,1024]{2,1,0:T(8,128)(2,1)} %bitcast.7, bf16[6,128,1024]{2,1,0:T(8,128)(2,1)} %bitcast.8, bf16[6,128,1024]{2,1,0:T(8,128)(2,1)} %bitcast.9, bf16[6,128,1024]{2,1,0:T(8,128)(2,1)} %bitcast.10, bf16[1024,1024]{1,0:T(8,128)(2,1)} %w_hbm.1, s32[1,4]{1,0:T(1,128)} %near_ref.1, ...), custom_call_target="tpu_custom_call" | custom-call | tf_op jit(solution)/shard_map/band_attention/pallas_call | solution.py:454
  81.6 1.1 %copy.11 = bf16[1,768,1024]{2,1,0:T(8,128)(2,1)} copy(bf16[1,768,1024]{2,1,0:T(8,128)(2,1)S(1)} %bitcast.6) | data formatting | bytes 3145728

commit v4 on v3

--- a/solution.py
+++ b/solution.py
@@ -28,7 +28,7 @@
     return CUTS[kind]
 
 
-def kernel(cfg, q_hbm, k_hbm, v_hbm, r_hbm, w_hbm, near_ref, start_ref, block_ref, count_ref, out_ref, *scratch):
+def kernel(cfg, q_hbm, k_hbm, v_hbm, r_hbm, w_hbm, near_hbm, start_hbm, block_hbm, count_hbm, out_ref, *scratch):
     cameras, rigs, chunks, qblocks, most, head_dim = cfg
     relay = relays(cameras, rigs)
     take = iter(scratch)
@@ -39,6 +39,7 @@
     ]
     q_ref, own_k, own_v, r_ref, w_ref, probs_ref, att_ref, acc_ref, own_sem = [next(take) for _ in range(9)]
     first_send, first_recv = next(take), next(take)
+    near_ref, start_ref, block_ref, count_ref, table_sem = [next(take) for _ in range(5)]
     if relay:
         mixed_ref, near_sem, far_sem, told_near, told_start, tell_send, tell_recv = [next(take) for _ in range(7)]
         x_send, z_send, b_send, z_recv, b_recv, x_recv = [next(take) for _ in range(6)]
@@ -79,7 +80,13 @@
             ((k_hbm, own_k), (v_hbm, own_v), (q_hbm, q_ref), (w_hbm, w_ref), (r_hbm, r_ref))
         )
     ]
-    for copy in loads[:2]:
+    tables = [
+        pltpu.make_async_copy(src, dst, table_sem.at[n])
+        for n, (src, dst) in enumerate(
+            ((near_hbm, near_ref), (start_hbm, start_ref), (block_hbm, block_ref), (count_hbm, count_ref))
+        )
+    ]
+    for copy in tables + loads[:2]:
         copy.start()
 
     def signal(sem, peer):
@@ -163,17 +170,6 @@
             return carry
 
         lax.fori_loop(0, count, step, 0, unroll=unroll)
-
-    slots = []
-    for view in views:
-        slot = jnp.int32(0)
-        for s in range(1, ROLES):
-            slot = jnp.where(near_ref[0, s] == view, s, slot)
-        slots.append(slot)
-    starts = [start_ref[0, slot] for slot in slots]
-    if relay:
-        starts[part_z] = jnp.int32(0)
-        starts[part_b] = jnp.where(from_x, 0, starts[part_b])
 
     def listed(r, b, m):
         index = starts[r] + block_ref[0, slots[r], m, b]
@@ -270,6 +266,18 @@
         for g in range(chunks):
             for kind in range(2):
                 first_copy(lane, g, kind).start()
+    for copy in tables:
+        copy.wait()
+    slots = []
+    for view in views:
+        slot = jnp.int32(0)
+        for s in range(1, ROLES):
+            slot = jnp.where(near_ref[0, s] == view, s, slot)
+        slots.append(slot)
+    starts = [start_ref[0, slot] for slot in slots]
+    if relay:
+        starts[part_z] = jnp.int32(0)
+        starts[part_b] = jnp.where(from_x, 0, starts[part_b])
 
     def first_wait(g, kind):
         for lane in range(len(first)):
@@ -376,9 +384,10 @@
             elif kind == 0:
                 n = len(cuts(cfg, part_x, g, kind))
                 run(score, g - 1, 0, part * qblocks // n, (part + 1) * qblocks // n, 3)
-            elif part >= len(cuts(cfg, part_x, g, kind)) - 2:
-                n = part - len(cuts(cfg, part_x, g, kind)) + 2
-                run(mix, g - 1, 1, n * qblocks // 2, (n + 1) * qblocks // 2, 3)
+            elif part in MIX_AFTER:
+                n = MIX_AFTER.index(part)
+                size = qblocks // len(MIX_AFTER)
+                run(mix, g - 1, 1, n * size, (n + 1) * size, 3)
         run(score, end, 0, 0, qblocks)
         first_wait(end, 1)
         each(lambda b: early(end, b), qblocks, LAST)
@@ -422,7 +431,6 @@
     lanes = 1 if relay else ROLES
     dma = pltpu.SemaphoreType.DMA
     anywhere = pl.BlockSpec(memory_space=pltpu.HBM)
-    scalars = pl.BlockSpec(memory_space=pltpu.SMEM)
     block_len = tokens // qblocks
     blocks = (qblocks, block_len, width)
     heads = LANES // head_dim
@@ -444,6 +452,8 @@
         dma((lanes, chunks, 2)),
         dma((lanes, chunks, 2)),
     ]
+    tables = (neighbours, band_start, jnp.swapaxes(band_blocks, 2, 3), band_count)
+    scratch += [pltpu.SMEM(table.shape, table.dtype) for table in tables] + [dma((4,))]
     if relay:
         scratch += [pltpu.VMEM((qblocks, heads * block_len, LANES), jnp.float32), regular, regular, pltpu.SMEM((2, 1, ROLES), jnp.int32), pltpu.SMEM((2, 1, ROLES), jnp.int32), dma((2, 2)), dma((2, 2))]
         scratch += [dma((chunks, 2))] * 5 + [dma((chunks, 2, max(len(c) for c in CUTS)))]
@@ -454,7 +464,7 @@
     out = pl.pallas_call(
         functools.partial(kernel, cfg),
         out_shape=pltpu.VMEM(blocks, bf16),
-        in_specs=[anywhere] * 5 + [scalars] * 4,
+        in_specs=[anywhere] * 9,
         out_specs=pl.BlockSpec(memory_space=pltpu.VMEM),
         scratch_shapes=scratch,
         compiler_params=pltpu.CompilerParams(
@@ -463,7 +473,7 @@
         name="band_attention",
     )(
         *(x[0].reshape(blocks) for x in (queries, keys, values, residual)),
-        w_out, neighbours, band_start, jnp.swapaxes(band_blocks, 2, 3), band_count,
+        w_out, *tables,
     )
     return out.reshape(tokens, width)[None]
 
@@ -473,6 +483,7 @@
 LAST = 6
 GROUP = 3
 TAIL = 6
+MIX_AFTER = (1, 3)
 TAIL_UNROLL = 1
 
 

time: 82.9 us -> 82.1 us (level)
  no operation moved by 1% of the time
where the time goes in v4:
time: 82.1 us; the launch traced here: 82 us
  Pallas kernels  80.8 us (98%)
  local copies, waits for them, and re-layouts  1.15 us (1%)
    pallas_call x1, Pallas kernels, per_device(): pl.pallas_call(functools.partial(kernel, cfg), out_shape=pltpu.VMEM(block...  80.8 us

profile of v4, /device:TPU:0, one launch (start us, length us, event | category | flops | bytes accessed | tf_op | source)
XLA Modules:
  0.0 82.0 jit_solution(5587346107366446591)
XLA Ops:
  0.0 80.8 %band_attention.1 = bf16[6,128,1024]{2,1,0:T(8,128)(2,1)S(1)} custom-call(bf16[6,128,1024]{2,1,0:T(8,128)(2,1)} %bitcast.7, bf16[6,128,1024]{2,1,0:T(8,128)(2,1)} %bitcast.8, bf16[6,128,1024]{2,1,0:T(8,128)(2,1)} %bitcast.9, bf16[6,128,1024]{2,1,0:T(8,128)(2,1)} %bitcast.10, bf16[1024,1024]{1,0:T(8,128)(2,1)} %w_hbm.1, s32[1,4]{1,0:T(1,128)} %near_hbm.1, ...), custom_call_target="tpu_custom_call" | custom-call | tf_op jit(solution)/shard_map/band_attention/pallas_call | solution.py:464
  80.8 1.1 %copy.11 = bf16[1,768,1024]{2,1,0:T(8,128)(2,1)} copy(bf16[1,768,1024]{2,1,0:T(8,128)(2,1)S(1)} %bitcast.6) | data formatting | bytes 3145728

commit v5 on v4

--- a/solution.py
+++ b/solution.py
@@ -39,7 +39,7 @@
     ]
     q_ref, own_k, own_v, r_ref, w_ref, probs_ref, att_ref, acc_ref, own_sem = [next(take) for _ in range(9)]
     first_send, first_recv = next(take), next(take)
-    near_ref, start_ref, block_ref, count_ref, table_sem = [next(take) for _ in range(5)]
+    near_ref, start_ref, block_ref, count_ref, table_sem, head_ref = [next(take) for _ in range(6)]
     if relay:
         mixed_ref, near_sem, far_sem, told_near, told_start, tell_send, tell_recv = [next(take) for _ in range(7)]
         x_send, z_send, b_send, z_recv, b_recv, x_recv = [next(take) for _ in range(6)]
@@ -86,7 +86,8 @@
             ((near_hbm, near_ref), (start_hbm, start_ref), (block_hbm, block_ref), (count_hbm, count_ref))
         )
     ]
-    for copy in tables + loads[:2]:
+    head = pltpu.make_async_copy(k_hbm.at[:, :, :LANES], head_ref, table_sem.at[4])
+    for copy in [head] + tables + loads[:2]:
         copy.start()
 
     def signal(sem, peer):
@@ -136,9 +137,12 @@
         return pl.ds(sum(sizes[:part]), sizes[part])
 
     def x_copy(g, kind, part):
-        source = own if g else (k_hbm, v_hbm)
+        if g == kind == 0:
+            source = head_ref.at[:, rows(g, kind, part)]
+        else:
+            source = (own if g else (k_hbm, v_hbm))[kind].at[:, rows(g, kind, part), cols(g)]
         return remote(
-            source[kind].at[:, rows(g, kind, part), cols(g)], near[kind][part_x][g][part],
+            source, near[kind][part_x][g][part],
             x_send.at[g, kind], x_recv.at[g, kind, part], across,
         )
 
@@ -250,6 +254,7 @@
         each(lambda group: project(g, group, count), qblocks // count)
 
     parts = [(g, kind, part) for g in range(chunks) for kind in range(2) for part in range(len(cuts(cfg, part_x, g, kind)))]
+    head.wait()
     if relay:
         for g, kind, part in parts:
             if g == 0:
@@ -453,7 +458,7 @@
         dma((lanes, chunks, 2)),
     ]
     tables = (neighbours, band_start, jnp.swapaxes(band_blocks, 2, 3), band_count)
-    scratch += [pltpu.SMEM(table.shape, table.dtype) for table in tables] + [dma((4,))]
+    scratch += [pltpu.SMEM(table.shape, table.dtype) for table in tables] + [dma((5,)), pltpu.VMEM((qblocks, block_len, LANES), bf16)]
     if relay:
         scratch += [pltpu.VMEM((qblocks, heads * block_len, LANES), jnp.float32), regular, regular, pltpu.SMEM((2, 1, ROLES), jnp.int32), pltpu.SMEM((2, 1, ROLES), jnp.int32), dma((2, 2)), dma((2, 2))]
         scratch += [dma((chunks, 2))] * 5 + [dma((chunks, 2, max(len(c) for c in CUTS)))]

time: 82.1 us -> 81.9 us (level)
  no operation moved by 1% of the time
where the time goes in v5:
time: 81.9 us; the launch traced here: 81.7 us
  Pallas kernels  80.6 us (98%)
  local copies, waits for them, and re-layouts  1.15 us (1%)
    pallas_call x1, Pallas kernels, per_device(): pl.pallas_call(functools.partial(kernel, cfg), out_shape=pltpu.VMEM(block...  80.6 us

profile of v5, /device:TPU:0, one launch (start us, length us, event | category | flops | bytes accessed | tf_op | source)
XLA Modules:
  0.0 81.7 jit_solution(2102787874760319339)
XLA Ops:
  0.0 80.6 %band_attention.1 = bf16[6,128,1024]{2,1,0:T(8,128)(2,1)S(1)} custom-call(bf16[6,128,1024]{2,1,0:T(8,128)(2,1)} %bitcast.7, bf16[6,128,1024]{2,1,0:T(8,128)(2,1)} %bitcast.8, bf16[6,128,1024]{2,1,0:T(8,128)(2,1)} %bitcast.9, bf16[6,128,1024]{2,1,0:T(8,128)(2,1)} %bitcast.10, bf16[1024,1024]{1,0:T(8,128)(2,1)} %w_hbm.1, s32[1,4]{1,0:T(1,128)} %near_hbm.1, ...), custom_call_target="tpu_custom_call" | custom-call | tf_op jit(solution)/shard_map/band_attention/pallas_call | solution.py:469
  80.6 1.1 %copy.11 = bf16[1,768,1024]{2,1,0:T(8,128)(2,1)} copy(bf16[1,768,1024]{2,1,0:T(8,128)(2,1)S(1)} %bitcast.6) | data formatting | bytes 3145728
